TPU v7x, 32 devices: a whole 2x2x4 slice. The times are simulated.
32 devices in a mesh: tm: 8 (over z, x), gz: 4 (over y, core).
Axes of the slice: x: 2, y: 2, z: 4, core: 2. Of those that a mesh axis runs over, the one named last changes fastest.
Arguments:
- source: float32 [16, 32, 32, 512], P('tm', None, None, 'gz'), may hold values from -8 to 8
- initial_guess: float32 [16, 32, 32, 512], P('tm', None, None, 'gz'), may hold values from -8 to 8
- diffusivity: float32 [32, 32, 512], P(None, None, 'gz'), may hold values from 0.25 to 2.5
Outputs:
- solution: float32 [16, 32, 32, 512], P('tm', None, None, 'gz')
- residual: float32 [16, 32, 32, 512], P('tm', None, None, 'gz')
All inputs are finite; a program needn't handle non-finite values.
Results may differ from a plain program's by a relative error of at most 0.00002.
Values sent between devices are 32-bit elements; how exact they have to be, the bound alone decides.
A program may use at most 128 MiB of HBM per device.

v0:
```python
import jax
import jax.numpy as jnp
from jax import lax
from jax.sharding import PartitionSpec as P

LEVELS = 5
SWEEPS = 2
CSWEEPS = 4


damping = 0.8
base_coef = 8.0


def passed_along(block, axis, distance):
    devices = range(lax.axis_size(axis))
    route = [(i - distance, i) for i in devices if i - distance in devices]
    return lax.ppermute(block, axis, route)


def padded_2(block, sides, width):
    for axis, dim in sides:
        count = lax.axis_size(axis)
        forward = [(i, i + 1) for i in range(count - 1)]
        backward = [(target, source) for source, target in forward]
        low = lax.ppermute(
            lax.slice_in_dim(block, block.shape[dim] - width, None, axis=dim), axis, forward
        )
        high = lax.ppermute(lax.slice_in_dim(block, 0, width, axis=dim), axis, backward)
        block = jnp.concatenate([low, block, high], axis=dim)
    return block


def partner(block, axis, distance):
    count = lax.axis_size(axis)
    route = []
    for low in range(count):
        high = low | 1 << distance
        if high != low and high < count:
            route += [(low, high), (high, low)]
    return lax.ppermute(block, axis, route)


def neighbours(padded):
    beside = padded[:, 2:, 1:-1, 1:-1] + padded[:, :-2, 1:-1, 1:-1]
    beside = beside + padded[:, 1:-1, 2:, 1:-1] + padded[:, 1:-1, :-2, 1:-1]
    beside = beside + padded[:, 1:-1, 1:-1, 2:] + padded[:, 1:-1, 1:-1, :-2]
    return beside


def operate(values, diffusivity, time_coef, stride):
    earlier = passed_along(values[-1:], "tm", stride)
    before = jnp.concatenate([earlier, values[:-1]], axis=0)
    padded = padded_2(values, (("gz", 3),), 1)
    padded = jnp.pad(padded, ((0, 0), (1, 1), (1, 1), (0, 0)))
    return time_coef * (values - before) + diffusivity * (6.0 * values - neighbours(padded))


def smooth_single(values, target, diffusivity, time_coef, stride, sweep_count):
    scaled = damping / (time_coef + 6.0 * diffusivity)
    for sweep_num in range(sweep_count):
        values = values + scaled * (target - operate(values, diffusivity, time_coef, stride))
    return values


def smooth(values, target, diffusivity, time_coef, stride, sweep_count):
    return smooth_single(values, target, diffusivity, time_coef, stride, sweep_count)


def cycle(level_num, values, target, diffusivity, coeff_wide, stride):
    time_coef = base_coef / 2.0**level_num
    if level_num == LEVELS - 1:
        return smooth(values, target, diffusivity, time_coef, stride, CSWEEPS)
    values = smooth(values, target, diffusivity, time_coef, stride, SWEEPS)
    leftover = target - operate(values, diffusivity, time_coef, stride)
    if values.shape[0] > 1:
        coarse_res = (leftover[0::2] + leftover[1::2]) * 0.5
        correction = cycle(
            level_num + 1, jnp.zeros_like(coarse_res), coarse_res, diffusivity, coeff_wide, stride
        )
        values = values + jnp.repeat(correction, 2, axis=0)
    else:
        other_res = partner(leftover, "tm", stride.bit_length() - 1)
        coarse_res = (leftover + other_res) * 0.5
        correction = cycle(
            level_num + 1,
            jnp.zeros_like(coarse_res),
            coarse_res,
            diffusivity,
            coeff_wide,
            2 * stride,
        )
        values = values + correction
    return smooth(values, target, diffusivity, time_coef, stride, SWEEPS)


def body(source, initial_guess, diffusivity):
    solution = cycle(0, initial_guess, source, diffusivity, diffusivity, 1)
    residual = source - operate(solution, diffusivity, base_coef, 1)
    return (solution, residual)


def solution(mesh):
    placed = (P("tm", None, None, "gz"), P("tm", None, None, "gz"), P(None, None, "gz"))
    return jax.shard_map(
        body,
        mesh=mesh,
        in_specs=placed,
        out_specs=(P("tm", None, None, "gz"), P("tm", None, None, "gz")),
        check_vma=False,
    )
```

profile of v0, /device:TPU:1, one launch (start us, length us, event | category | flops | bytes accessed | tf_op | source)
XLA Modules:
  0.0 507.6 jit_solution(3973345104033796954)
XLA Ops:
  5.3 4.5 collective-permute-start.1
  13.3 3.9 collective-permute-start
  21.7 5.3 %collective-permute-done = f32[1,32,32,128]{3,2,1,0:T(8,128)} collective-permute-done((f32[1,32,32,128]{3,2,1,0:T(8,128)}, f32[1,32,32,128]{3,2,1,0:T(8,128)}, u32[]{:S(2)}, u32[]{:S(2)}) %collective-permute-start) | collective-permute-done | bytes 524320 | tf_op jit(solution)/shard_map/ppermute | solution.py:18
  31.5 4.6 collective-permute-start.3
  39.2 4.3 collective-permute-start.4
  46.7 3.6 collective-permute-start.10
  53.2 4.0 collective-permute-start.9
  69.2 3.9 collective-permute-start.7
  92.7 4.1 collective-permute-start.12
  97.0 4.3 collective-permute-start.13
  103.2 4.2 collective-permute-done.13
  107.4 4.4 collective-permute-done.14
  113.5 5.0 collective-permute-start.15
  126.8 4.7 collective-permute-done.17
  133.2 4.9 collective-permute-done.19
  138.1 3.7 collective-permute-done.18
  142.1 5.3 %collective-permute-start.20 = (f32[1,32,32,128]{3,2,1,0:T(8,128)S(1)}, f32[1,32,32,128]{3,2,1,0:T(8,128)S(1)}, u32[]{:S(2)}, u32[]{:S(2)}) collective-permute-start(f32[1,32,32,128]{3,2,1,0:T(8,128)S(1)} %get-tuple-element.8), channel_id=1, source_target_pairs={{0,8},{4,12},{8,16},{12,20},{16,24},{20,28},{1,9},{5,13},{9,17},{1... | collective-permute-start | bytes 1572872 | tf_op jit(solution)/shard_map/ppermute | solution.py:18
  155.6 4.4 collective-permute-done.22
  173.3 4.4 collective-permute-done.25
  179.6 7.2 %collective-permute-done.27 = f32[1,32,32,128]{3,2,1,0:T(8,128)S(1)} collective-permute-done((f32[1,32,32,128]{3,2,1,0:T(8,128)}, f32[1,32,32,128]{3,2,1,0:T(8,128)S(1)}, u32[]{:S(2)}, u32[]{:S(2)}) %collective-permute-start.27) | collective-permute-done | bytes 524320 | tf_op jit(solution)/shard_map/ppermute | solution.py:18
  186.8 6.5 %collective-permute-done.26 = f32[1,32,32,128]{3,2,1,0:T(8,128)S(1)} collective-permute-done((f32[1,32,32,128]{3,2,1,0:T(8,128)S(1)}, f32[1,32,32,128]{3,2,1,0:T(8,128)S(1)}, u32[]{:S(2)}, u32[]{:S(2)}) %collective-permute-start.26) | collective-permute-done | bytes 524320 | tf_op jit(solution)/shard_map/ppermute | solution.py:41
  195.2 5.3 %collective-permute-start.29 = (f32[1,32,32,1]{3,2,1,0:T(8,128)S(1)}, f32[1,32,32,1]{3,2,1,0:T(8,128)S(1)}, u32[]{:S(2)}, u32[]{:S(2)}) collective-permute-start(f32[1,32,32,1]{3,2,1,0:T(8,128)S(1)} %get-tuple-element.58), channel_id=1, source_target_pairs={{0,1},{1,2},{2,3},{4,5},{5,6},{6,7},{8,9},{9,10},{10,11},{12,13},{... | collective-permute-start | bytes 12296 | tf_op jit(solution)/shard_map/ppermute | solution.py:26
  200.5 11.6 %collective-permute-start.30 = (f32[1,32,32,1]{3,2,1,0:T(8,128)S(1)}, f32[1,32,32,1]{3,2,1,0:T(8,128)S(1)}, u32[]{:S(2)}, u32[]{:S(2)}) collective-permute-start(f32[1,32,32,1]{3,2,1,0:T(8,128)S(1)} %get-tuple-element.57), channel_id=1, source_target_pairs={{1,0},{2,1},{3,2},{5,4},{6,5},{7,6},{9,8},{10,9},{11,10},{13,12},{... | collective-permute-start | bytes 12296 | tf_op jit(solution)/shard_map/ppermute | solution.py:29
  218.7 6.5 %collective-permute-start.33 = (f32[1,32,32,1]{3,2,1,0:T(8,128)S(1)}, f32[1,32,32,1]{3,2,1,0:T(8,128)S(1)}, u32[]{:S(2)}, u32[]{:S(2)}) collective-permute-start(f32[1,32,32,1]{3,2,1,0:T(8,128)S(1)} %get-tuple-element.55), channel_id=1, source_target_pairs={{1,0},{2,1},{3,2},{5,4},{6,5},{7,6},{9,8},{10,9},{11,10},{13,12},{... | collective-permute-start | bytes 12296 | tf_op jit(solution)/shard_map/ppermute | solution.py:29
  230.9 14.5 %collective-permute-done.34 = f32[1,32,32,128]{3,2,1,0:T(8,128)S(1)} collective-permute-done((f32[1,32,32,128]{3,2,1,0:T(8,128)S(1)}, f32[1,32,32,128]{3,2,1,0:T(8,128)S(1)}, u32[]{:S(2)}, u32[]{:S(2)}) %collective-permute-start.34) | collective-permute-done | bytes 524320 | tf_op jit(solution)/shard_map/ppermute | solution.py:41
  251.1 3.7 collective-permute-done.37
  254.7 4.4 collective-permute-done.38
  266.3 3.5 collective-permute-done.40
  269.8 4.4 collective-permute-done.41
  281.1 3.7 collective-permute-done.43
  284.8 4.4 collective-permute-done.44
  296.8 3.8 collective-permute-done.46
  300.6 4.4 collective-permute-done.47
  312.6 3.7 collective-permute-done.49
  316.2 4.4 collective-permute-done.50
  322.3 33.1 %collective-permute-start.51 = (f32[1,32,32,128]{3,2,1,0:T(8,128)S(1)}, f32[1,32,32,128]{3,2,1,0:T(8,128)S(1)}, u32[]{:S(2)}, u32[]{:S(2)}) collective-permute-start(f32[1,32,32,128]{3,2,1,0:T(8,128)S(1)} %fusion.101), channel_id=1, source_target_pairs={{0,8},{4,12},{8,16},{12,20},{16,24},{20,28},{1,9},{5,13},{9,17},{1... | collective-permute-start | bytes 1572872 | tf_op jit(solution)/shard_map/ppermute | solution.py:18
  360.0 3.8 collective-permute-done.52
  363.8 4.4 collective-permute-done.53
  376.5 3.6 collective-permute-done.55
  380.0 4.4 collective-permute-done.56
  386.1 19.9 %collective-permute-start.57 = (f32[1,32,32,128]{3,2,1,0:T(8,128)S(1)}, f32[1,32,32,128]{3,2,1,0:T(8,128)S(1)}, u32[]{:S(2)}, u32[]{:S(2)}) collective-permute-start(f32[1,32,32,128]{3,2,1,0:T(8,128)S(1)} %fusion.84), channel_id=1, source_target_pairs={{0,4},{4,8},{8,12},{12,16},{16,20},{20,24},{24,28},{1,5},{5,9},{9,... | collective-permute-start | bytes 1572872 | tf_op jit(solution)/shard_map/ppermute | solution.py:18
  410.6 3.8 collective-permute-done.58
  414.4 4.4 collective-permute-done.59
  426.9 3.8 collective-permute-done.61
  430.6 4.4 collective-permute-done.62
  438.0 3.8 collective-permute-start.63
  478.1 4.3 fusion.18
  503.1 4.0 fusion.10
  (250 shorter events, 232.3 us)
Async XLA Ops:
  5.3 12.0 %collective-permute-start.1 = (f32[2,32,32,1]{2,1,3,0:T(8,128)S(1)}, f32[2,32,32,1]{2,1,3,0:T(8,128)S(1)}, u32[]{:S(2)}, u32[]{:S(2)}) collective-permute-start(f32[2,32,32,1]{2,1,3,0:T(8,128)S(1)} %copy.62), channel_id=1, source_target_pairs={{0,1},{1,2},{2,3},{4,5},{5,6},{6,7},{8,9},{9,10},{10,11},{12,13},{... | collective-permute-start | bytes 24584 | tf_op jit(solution)/shard_map/ppermute | solution.py:26
  13.3 13.7 %collective-permute-start = (f32[1,32,32,128]{3,2,1,0:T(8,128)}, f32[1,32,32,128]{3,2,1,0:T(8,128)}, u32[]{:S(2)}, u32[]{:S(2)}) collective-permute-start(f32[1,32,32,128]{3,2,1,0:T(8,128)} %get-tuple-element.33), channel_id=1, source_target_pairs={{0,4},{4,8},{8,12},{12,16},{16,20},{20,24},{24,28},{1,5},{5,9},{9,... | collective-permute-start | bytes 1572872 | tf_op jit(solution)/shard_map/ppermute | solution.py:18
  31.5 30.1 %collective-permute-start.3 = (f32[1,32,32,128]{3,2,1,0:T(8,128)}, f32[1,32,32,128]{3,2,1,0:T(8,128)}, u32[]{:S(2)}, u32[]{:S(2)}) collective-permute-start(f32[1,32,32,128]{3,2,1,0:T(8,128)} %get-tuple-element.29), channel_id=1, source_target_pairs={{0,4},{4,8},{8,12},{12,16},{16,20},{20,24},{24,28},{1,5},{5,9},{9,... | collective-permute-start | bytes 1572872 | tf_op jit(solution)/shard_map/ppermute | solution.py:18
  39.2 13.1 %collective-permute-start.4 = (f32[2,32,32,1]{2,1,3,0:T(8,128)S(1)}, f32[2,32,32,1]{2,1,3,0:T(8,128)S(1)}, u32[]{:S(2)}, u32[]{:S(2)}) collective-permute-start(f32[2,32,32,1]{2,1,3,0:T(8,128)S(1)} %copy.32), channel_id=1, source_target_pairs={{0,1},{1,2},{2,3},{4,5},{5,6},{6,7},{8,9},{9,10},{10,11},{12,13},{... | collective-permute-start | bytes 24584 | tf_op jit(solution)/shard_map/ppermute | solution.py:26
  43.9 13.7 %collective-permute-start.5 = (f32[2,32,32,1]{2,1,3,0:T(8,128)S(1)}, f32[2,32,32,1]{2,1,3,0:T(8,128)S(1)}, u32[]{:S(2)}, u32[]{:S(2)}) collective-permute-start(f32[2,32,32,1]{2,1,3,0:T(8,128)S(1)} %copy.33), channel_id=1, source_target_pairs={{1,0},{2,1},{3,2},{5,4},{6,5},{7,6},{9,8},{10,9},{11,10},{13,12},{... | collective-permute-start | bytes 24584 | tf_op jit(solution)/shard_map/ppermute | solution.py:29
  46.7 28.7 %collective-permute-start.10 = (f32[1,32,32,1]{3,2,1,0:T(8,128)}, f32[1,32,32,1]{3,2,1,0:T(8,128)}, u32[]{:S(2)}, u32[]{:S(2)}) collective-permute-start(f32[1,32,32,1]{3,2,1,0:T(8,128)} %broadcast.103), channel_id=1, source_target_pairs={{0,1},{1,2},{2,3},{4,5},{5,6},{6,7},{8,9},{9,10},{10,11},{12,13},{... | collective-permute-start | bytes 12296 | tf_op jit(solution)/shard_map/ppermute | solution.py:26
  50.4 27.6 %collective-permute-start.11 = (f32[1,32,32,1]{3,2,1,0:T(8,128)}, f32[1,32,32,1]{3,2,1,0:T(8,128)}, u32[]{:S(2)}, u32[]{:S(2)}) collective-permute-start(f32[1,32,32,1]{3,2,1,0:T(8,128)} %broadcast.103), channel_id=1, source_target_pairs={{1,0},{2,1},{3,2},{5,4},{6,5},{7,6},{9,8},{10,9},{11,10},{13,12},{... | collective-permute-start | bytes 12296 | tf_op jit(solution)/shard_map/ppermute | solution.py:29
  53.2 37.3 %collective-permute-start.9 = (f32[1,32,32,128]{3,2,1,0:T(8,128)}, f32[1,32,32,128]{3,2,1,0:T(8,128)}, u32[]{:S(2)}, u32[]{:S(2)}) collective-permute-start(f32[1,32,32,128]{3,2,1,0:T(8,128)} %broadcast.101), channel_id=1, source_target_pairs={{0,4},{4,8},{8,12},{12,16},{16,20},{20,24},{24,28},{1,5},{5,9},{9,... | collective-permute-start | bytes 1572872 | tf_op jit(solution)/shard_map/ppermute | solution.py:18
  69.2 11.8 %collective-permute-start.7 = (f32[2,32,32,1]{2,1,3,0:T(8,128)S(1)}, f32[2,32,32,1]{2,1,3,0:T(8,128)S(1)}, u32[]{:S(2)}, u32[]{:S(2)}) collective-permute-start(f32[2,32,32,1]{2,1,3,0:T(8,128)S(1)} %copy.38), channel_id=1, source_target_pairs={{0,1},{1,2},{2,3},{4,5},{5,6},{6,7},{8,9},{9,10},{10,11},{12,13},{... | collective-permute-start | bytes 24584 | tf_op jit(solution)/shard_map/ppermute | solution.py:26
  75.5 11.8 %collective-permute-start.6 = (f32[1,32,32,128]{3,2,1,0:T(8,128)}, f32[1,32,32,128]{3,2,1,0:T(8,128)}, u32[]{:S(2)}, u32[]{:S(2)}) collective-permute-start(f32[1,32,32,128]{3,2,1,0:T(8,128)} %get-tuple-element.25), channel_id=1, source_target_pairs={{0,4},{4,8},{8,12},{12,16},{16,20},{20,24},{24,28},{1,5},{5,9},{9,... | collective-permute-start | bytes 1572872 | tf_op jit(solution)/shard_map/ppermute | solution.py:18
  92.7 19.7 %collective-permute-start.12 = (f32[1,32,32,128]{3,2,1,0:T(8,128)S(1)}, f32[1,32,32,128]{3,2,1,0:T(8,128)S(1)}, u32[]{:S(2)}, u32[]{:S(2)}) collective-permute-start(f32[1,32,32,128]{3,2,1,0:T(8,128)S(1)} %get-tuple-element.10), channel_id=1, source_target_pairs={{0,4},{4,8},{8,12},{12,16},{16,20},{20,24},{24,28},{1,5},{5,9},{9,... | collective-permute-start | bytes 1572872 | tf_op jit(solution)/shard_map/ppermute | solution.py:18
  101.3 10.5 %collective-permute-start.14 = (f32[1,32,32,1]{3,2,1,0:T(8,128)S(1)}, f32[1,32,32,1]{3,2,1,0:T(8,128)S(1)}, u32[]{:S(2)}, u32[]{:S(2)}) collective-permute-start(f32[1,32,32,1]{3,2,1,0:T(8,128)S(1)} %get-tuple-element.65), channel_id=1, source_target_pairs={{1,0},{2,1},{3,2},{5,4},{6,5},{7,6},{9,8},{10,9},{11,10},{13,12},{... | collective-permute-start | bytes 12296 | tf_op jit(solution)/shard_map/ppermute | solution.py:29
  113.5 18.6 %collective-permute-start.15 = (f32[1,32,32,128]{3,2,1,0:T(8,128)S(1)}, f32[1,32,32,128]{3,2,1,0:T(8,128)S(1)}, u32[]{:S(2)}, u32[]{:S(2)}) collective-permute-start(f32[1,32,32,128]{3,2,1,0:T(8,128)S(1)} %fusion.176), channel_id=1, source_target_pairs={{0,4},{4,8},{8,12},{12,16},{16,20},{20,24},{24,28},{1,5},{5,9},{9,... | collective-permute-start | bytes 1572872 | tf_op jit(solution)/shard_map/ppermute | solution.py:18
  120.7 10.8 %collective-permute-start.17 = (f32[1,32,32,1]{3,2,1,0:T(8,128)S(1)}, f32[1,32,32,1]{3,2,1,0:T(8,128)S(1)}, u32[]{:S(2)}, u32[]{:S(2)}) collective-permute-start(f32[1,32,32,1]{3,2,1,0:T(8,128)S(1)} %get-tuple-element.63), channel_id=1, source_target_pairs={{1,0},{2,1},{3,2},{5,4},{6,5},{7,6},{9,8},{10,9},{11,10},{13,12},{... | collective-permute-start | bytes 12296 | tf_op jit(solution)/shard_map/ppermute | solution.py:29
  123.0 15.1 %collective-permute-start.19 = (f32[1,32,32,128]{3,2,1,0:T(8,128)}, f32[1,32,32,128]{3,2,1,0:T(8,128)S(1)}, u32[]{:S(2)}, u32[]{:S(2)}) collective-permute-start(f32[1,32,32,128]{3,2,1,0:T(8,128)} %broadcast.101), channel_id=1, source_target_pairs={{0,8},{4,12},{8,16},{12,20},{16,24},{20,28},{1,9},{5,13},{9,17},{1... | collective-permute-start | bytes 1572872 | tf_op jit(solution)/shard_map/ppermute | solution.py:18
  142.1 18.5 %collective-permute-start.20 = (f32[1,32,32,128]{3,2,1,0:T(8,128)S(1)}, f32[1,32,32,128]{3,2,1,0:T(8,128)S(1)}, u32[]{:S(2)}, u32[]{:S(2)}) collective-permute-start(f32[1,32,32,128]{3,2,1,0:T(8,128)S(1)} %get-tuple-element.8), channel_id=1, source_target_pairs={{0,8},{4,12},{8,16},{12,20},{16,24},{20,28},{1,9},{5,13},{9,17},{1... | collective-permute-start | bytes 1572872 | tf_op jit(solution)/shard_map/ppermute | solution.py:18
  149.5 10.5 %collective-permute-start.22 = (f32[1,32,32,1]{3,2,1,0:T(8,128)S(1)}, f32[1,32,32,1]{3,2,1,0:T(8,128)S(1)}, u32[]{:S(2)}, u32[]{:S(2)}) collective-permute-start(f32[1,32,32,1]{3,2,1,0:T(8,128)S(1)} %get-tuple-element.61), channel_id=1, source_target_pairs={{1,0},{2,1},{3,2},{5,4},{6,5},{7,6},{9,8},{10,9},{11,10},{13,12},{... | collective-permute-start | bytes 12296 | tf_op jit(solution)/shard_map/ppermute | solution.py:29
  161.7 16.6 %collective-permute-start.23 = (f32[1,32,32,128]{3,2,1,0:T(8,128)S(1)}, f32[1,32,32,128]{3,2,1,0:T(8,128)S(1)}, u32[]{:S(2)}, u32[]{:S(2)}) collective-permute-start(f32[1,32,32,128]{3,2,1,0:T(8,128)S(1)} %fusion.162), channel_id=1, source_target_pairs={{0,8},{4,12},{8,16},{12,20},{16,24},{20,28},{1,9},{5,13},{9,17},{1... | collective-permute-start | bytes 1572872 | tf_op jit(solution)/shard_map/ppermute | solution.py:18
  167.2 10.5 %collective-permute-start.25 = (f32[1,32,32,1]{3,2,1,0:T(8,128)S(1)}, f32[1,32,32,1]{3,2,1,0:T(8,128)S(1)}, u32[]{:S(2)}, u32[]{:S(2)}) collective-permute-start(f32[1,32,32,1]{3,2,1,0:T(8,128)S(1)} %get-tuple-element.59), channel_id=1, source_target_pairs={{1,0},{2,1},{3,2},{5,4},{6,5},{7,6},{9,8},{10,9},{11,10},{13,12},{... | collective-permute-start | bytes 12296 | tf_op jit(solution)/shard_map/ppermute | solution.py:29
  169.5 17.3 %collective-permute-start.27 = (f32[1,32,32,128]{3,2,1,0:T(8,128)}, f32[1,32,32,128]{3,2,1,0:T(8,128)S(1)}, u32[]{:S(2)}, u32[]{:S(2)}) collective-permute-start(f32[1,32,32,128]{3,2,1,0:T(8,128)} %broadcast.101), channel_id=1, source_target_pairs={{0,16},{4,20},{8,24},{12,28},{1,17},{5,21},{9,25},{13,29},{2,18},{... | collective-permute-start | bytes 1572872 | tf_op jit(solution)/shard_map/ppermute | solution.py:18
  179.3 14.0 %collective-permute-start.26 = (f32[1,32,32,128]{3,2,1,0:T(8,128)S(1)}, f32[1,32,32,128]{3,2,1,0:T(8,128)S(1)}, u32[]{:S(2)}, u32[]{:S(2)}) collective-permute-start(f32[1,32,32,128]{3,2,1,0:T(8,128)S(1)} %fusion.154), channel_id=1, source_target_pairs={{0,8},{8,0},{4,12},{12,4},{16,24},{24,16},{20,28},{28,20},{1,9},{9... | collective-permute-start | bytes 1572872 | tf_op jit(solution)/shard_map/ppermute | solution.py:41
  193.6 20.6 %collective-permute-start.28 = (f32[1,32,32,128]{3,2,1,0:T(8,128)S(1)}, f32[1,32,32,128]{3,2,1,0:T(8,128)S(1)}, u32[]{:S(2)}, u32[]{:S(2)}) collective-permute-start(f32[1,32,32,128]{3,2,1,0:T(8,128)S(1)} %get-tuple-element.6), channel_id=1, source_target_pairs={{0,16},{4,20},{8,24},{12,28},{1,17},{5,21},{9,25},{13,29},{2,18},{... | collective-permute-start | bytes 1572872 | tf_op jit(solution)/shard_map/ppermute | solution.py:18
  195.2 16.9 %collective-permute-start.29 = (f32[1,32,32,1]{3,2,1,0:T(8,128)S(1)}, f32[1,32,32,1]{3,2,1,0:T(8,128)S(1)}, u32[]{:S(2)}, u32[]{:S(2)}) collective-permute-start(f32[1,32,32,1]{3,2,1,0:T(8,128)S(1)} %get-tuple-element.58), channel_id=1, source_target_pairs={{0,1},{1,2},{2,3},{4,5},{5,6},{6,7},{8,9},{9,10},{10,11},{12,13},{... | collective-permute-start | bytes 12296 | tf_op jit(solution)/shard_map/ppermute | solution.py:26
  200.5 13.1 %collective-permute-start.30 = (f32[1,32,32,1]{3,2,1,0:T(8,128)S(1)}, f32[1,32,32,1]{3,2,1,0:T(8,128)S(1)}, u32[]{:S(2)}, u32[]{:S(2)}) collective-permute-start(f32[1,32,32,1]{3,2,1,0:T(8,128)S(1)} %get-tuple-element.57), channel_id=1, source_target_pairs={{1,0},{2,1},{3,2},{5,4},{6,5},{7,6},{9,8},{10,9},{11,10},{13,12},{... | collective-permute-start | bytes 12296 | tf_op jit(solution)/shard_map/ppermute | solution.py:29
  215.2 14.6 %collective-permute-start.31 = (f32[1,32,32,128]{3,2,1,0:T(8,128)S(1)}, f32[1,32,32,128]{3,2,1,0:T(8,128)S(1)}, u32[]{:S(2)}, u32[]{:S(2)}) collective-permute-start(f32[1,32,32,128]{3,2,1,0:T(8,128)S(1)} %fusion.148), channel_id=1, source_target_pairs={{0,16},{4,20},{8,24},{12,28},{1,17},{5,21},{9,25},{13,29},{2,18},{... | collective-permute-start | bytes 1572872 | tf_op jit(solution)/shard_map/ppermute | solution.py:18
  218.7 10.5 %collective-permute-start.33 = (f32[1,32,32,1]{3,2,1,0:T(8,128)S(1)}, f32[1,32,32,1]{3,2,1,0:T(8,128)S(1)}, u32[]{:S(2)}, u32[]{:S(2)}) collective-permute-start(f32[1,32,32,1]{3,2,1,0:T(8,128)S(1)} %get-tuple-element.55), channel_id=1, source_target_pairs={{1,0},{2,1},{3,2},{5,4},{6,5},{7,6},{9,8},{10,9},{11,10},{13,12},{... | collective-permute-start | bytes 12296 | tf_op jit(solution)/shard_map/ppermute | solution.py:29
  230.9 14.6 %collective-permute-start.34 = (f32[1,32,32,128]{3,2,1,0:T(8,128)S(1)}, f32[1,32,32,128]{3,2,1,0:T(8,128)S(1)}, u32[]{:S(2)}, u32[]{:S(2)}) collective-permute-start(f32[1,32,32,128]{3,2,1,0:T(8,128)S(1)} %fusion.140), channel_id=1, source_target_pairs={{0,16},{16,0},{4,20},{20,4},{8,24},{24,8},{12,28},{28,12},{1,17},{... | collective-permute-start | bytes 1572872 | tf_op jit(solution)/shard_map/ppermute | solution.py:41
  245.8 13.9 %collective-permute-start.36 = (f32[1,32,32,128]{3,2,1,0:T(8,128)S(1)}, f32[1,32,32,128]{3,2,1,0:T(8,128)S(1)}, u32[]{:S(2)}, u32[]{:S(2)}) collective-permute-start(f32[1,32,32,128]{3,2,1,0:T(8,128)S(1)} %get-tuple-element.4), channel_id=1, source_target_pairs={} | collective-permute-start | bytes 1572872 | tf_op jit(solution)/shard_map/ppermute | solution.py:18
  248.6 10.5 %collective-permute-start.38 = (f32[1,32,32,1]{3,2,1,0:T(8,128)S(1)}, f32[1,32,32,1]{3,2,1,0:T(8,128)S(1)}, u32[]{:S(2)}, u32[]{:S(2)}) collective-permute-start(f32[1,32,32,1]{3,2,1,0:T(8,128)S(1)} %get-tuple-element.53), channel_id=1, source_target_pairs={{1,0},{2,1},{3,2},{5,4},{6,5},{7,6},{9,8},{10,9},{11,10},{13,12},{... | collective-permute-start | bytes 12296 | tf_op jit(solution)/shard_map/ppermute | solution.py:29
  260.8 13.9 %collective-permute-start.39 = (f32[1,32,32,128]{3,2,1,0:T(8,128)S(1)}, f32[1,32,32,128]{3,2,1,0:T(8,128)S(1)}, u32[]{:S(2)}, u32[]{:S(2)}) collective-permute-start(f32[1,32,32,128]{3,2,1,0:T(8,128)S(1)} %fusion.134), channel_id=1, source_target_pairs={} | collective-permute-start | bytes 1572872 | tf_op jit(solution)/shard_map/ppermute | solution.py:18
  263.7 10.5 %collective-permute-start.41 = (f32[1,32,32,1]{3,2,1,0:T(8,128)S(1)}, f32[1,32,32,1]{3,2,1,0:T(8,128)S(1)}, u32[]{:S(2)}, u32[]{:S(2)}) collective-permute-start(f32[1,32,32,1]{3,2,1,0:T(8,128)S(1)} %get-tuple-element.51), channel_id=1, source_target_pairs={{1,0},{2,1},{3,2},{5,4},{6,5},{7,6},{9,8},{10,9},{11,10},{13,12},{... | collective-permute-start | bytes 12296 | tf_op jit(solution)/shard_map/ppermute | solution.py:29
  275.8 13.9 %collective-permute-start.42 = (f32[1,32,32,128]{3,2,1,0:T(8,128)S(1)}, f32[1,32,32,128]{3,2,1,0:T(8,128)S(1)}, u32[]{:S(2)}, u32[]{:S(2)}) collective-permute-start(f32[1,32,32,128]{3,2,1,0:T(8,128)S(1)} %fusion.126), channel_id=1, source_target_pairs={} | collective-permute-start | bytes 1572872 | tf_op jit(solution)/shard_map/ppermute | solution.py:18
  278.7 10.5 %collective-permute-start.44 = (f32[1,32,32,1]{3,2,1,0:T(8,128)S(1)}, f32[1,32,32,1]{3,2,1,0:T(8,128)S(1)}, u32[]{:S(2)}, u32[]{:S(2)}) collective-permute-start(f32[1,32,32,1]{3,2,1,0:T(8,128)S(1)} %get-tuple-element.49), channel_id=1, source_target_pairs={{1,0},{2,1},{3,2},{5,4},{6,5},{7,6},{9,8},{10,9},{11,10},{13,12},{... | collective-permute-start | bytes 12296 | tf_op jit(solution)/shard_map/ppermute | solution.py:29
  290.9 14.7 %collective-permute-start.45 = (f32[1,32,32,128]{3,2,1,0:T(8,128)S(1)}, f32[1,32,32,128]{3,2,1,0:T(8,128)S(1)}, u32[]{:S(2)}, u32[]{:S(2)}) collective-permute-start(f32[1,32,32,128]{3,2,1,0:T(8,128)S(1)} %fusion.118), channel_id=1, source_target_pairs={{0,16},{4,20},{8,24},{12,28},{1,17},{5,21},{9,25},{13,29},{2,18},{... | collective-permute-start | bytes 1572872 | tf_op jit(solution)/shard_map/ppermute | solution.py:18
  294.5 10.5 %collective-permute-start.47 = (f32[1,32,32,1]{3,2,1,0:T(8,128)S(1)}, f32[1,32,32,1]{3,2,1,0:T(8,128)S(1)}, u32[]{:S(2)}, u32[]{:S(2)}) collective-permute-start(f32[1,32,32,1]{3,2,1,0:T(8,128)S(1)} %get-tuple-element.47), channel_id=1, source_target_pairs={{1,0},{2,1},{3,2},{5,4},{6,5},{7,6},{9,8},{10,9},{11,10},{13,12},{... | collective-permute-start | bytes 12296 | tf_op jit(solution)/shard_map/ppermute | solution.py:29
  306.7 14.6 %collective-permute-start.48 = (f32[1,32,32,128]{3,2,1,0:T(8,128)S(1)}, f32[1,32,32,128]{3,2,1,0:T(8,128)S(1)}, u32[]{:S(2)}, u32[]{:S(2)}) collective-permute-start(f32[1,32,32,128]{3,2,1,0:T(8,128)S(1)} %fusion.109), channel_id=1, source_target_pairs={{0,16},{4,20},{8,24},{12,28},{1,17},{5,21},{9,25},{13,29},{2,18},{... | collective-permute-start | bytes 1572872 | tf_op jit(solution)/shard_map/ppermute | solution.py:18
  310.1 10.5 %collective-permute-start.50 = (f32[1,32,32,1]{3,2,1,0:T(8,128)S(1)}, f32[1,32,32,1]{3,2,1,0:T(8,128)S(1)}, u32[]{:S(2)}, u32[]{:S(2)}) collective-permute-start(f32[1,32,32,1]{3,2,1,0:T(8,128)S(1)} %get-tuple-element.45), channel_id=1, source_target_pairs={{1,0},{2,1},{3,2},{5,4},{6,5},{7,6},{9,8},{10,9},{11,10},{13,12},{... | collective-permute-start | bytes 12296 | tf_op jit(solution)/shard_map/ppermute | solution.py:29
  322.3 46.5 %collective-permute-start.51 = (f32[1,32,32,128]{3,2,1,0:T(8,128)S(1)}, f32[1,32,32,128]{3,2,1,0:T(8,128)S(1)}, u32[]{:S(2)}, u32[]{:S(2)}) collective-permute-start(f32[1,32,32,128]{3,2,1,0:T(8,128)S(1)} %fusion.101), channel_id=1, source_target_pairs={{0,8},{4,12},{8,16},{12,20},{16,24},{20,28},{1,9},{5,13},{9,17},{1... | collective-permute-start | bytes 1572872 | tf_op jit(solution)/shard_map/ppermute | solution.py:18
  357.7 10.5 %collective-permute-start.53 = (f32[1,32,32,1]{3,2,1,0:T(8,128)S(1)}, f32[1,32,32,1]{3,2,1,0:T(8,128)S(1)}, u32[]{:S(2)}, u32[]{:S(2)}) collective-permute-start(f32[1,32,32,1]{3,2,1,0:T(8,128)S(1)} %get-tuple-element.43), channel_id=1, source_target_pairs={{1,0},{2,1},{3,2},{5,4},{6,5},{7,6},{9,8},{10,9},{11,10},{13,12},{... | collective-permute-start | bytes 12296 | tf_op jit(solution)/shard_map/ppermute | solution.py:29
  369.9 15.2 %collective-permute-start.54 = (f32[1,32,32,128]{3,2,1,0:T(8,128)S(1)}, f32[1,32,32,128]{3,2,1,0:T(8,128)S(1)}, u32[]{:S(2)}, u32[]{:S(2)}) collective-permute-start(f32[1,32,32,128]{3,2,1,0:T(8,128)S(1)} %fusion.92), channel_id=1, source_target_pairs={{0,8},{4,12},{8,16},{12,20},{16,24},{20,28},{1,9},{5,13},{9,17},{1... | collective-permute-start | bytes 1572872 | tf_op jit(solution)/shard_map/ppermute | solution.py:18
  373.9 10.5 %collective-permute-start.56 = (f32[1,32,32,1]{3,2,1,0:T(8,128)S(1)}, f32[1,32,32,1]{3,2,1,0:T(8,128)S(1)}, u32[]{:S(2)}, u32[]{:S(2)}) collective-permute-start(f32[1,32,32,1]{3,2,1,0:T(8,128)S(1)} %get-tuple-element.41), channel_id=1, source_target_pairs={{1,0},{2,1},{3,2},{5,4},{6,5},{7,6},{9,8},{10,9},{11,10},{13,12},{... | collective-permute-start | bytes 12296 | tf_op jit(solution)/shard_map/ppermute | solution.py:29
  386.1 33.3 %collective-permute-start.57 = (f32[1,32,32,128]{3,2,1,0:T(8,128)S(1)}, f32[1,32,32,128]{3,2,1,0:T(8,128)S(1)}, u32[]{:S(2)}, u32[]{:S(2)}) collective-permute-start(f32[1,32,32,128]{3,2,1,0:T(8,128)S(1)} %fusion.84), channel_id=1, source_target_pairs={{0,4},{4,8},{8,12},{12,16},{16,20},{20,24},{24,28},{1,5},{5,9},{9,... | collective-permute-start | bytes 1572872 | tf_op jit(solution)/shard_map/ppermute | solution.py:18
  408.3 10.5 %collective-permute-start.59 = (f32[1,32,32,1]{3,2,1,0:T(8,128)S(1)}, f32[1,32,32,1]{3,2,1,0:T(8,128)S(1)}, u32[]{:S(2)}, u32[]{:S(2)}) collective-permute-start(f32[1,32,32,1]{3,2,1,0:T(8,128)S(1)} %get-tuple-element.39), channel_id=1, source_target_pairs={{1,0},{2,1},{3,2},{5,4},{6,5},{7,6},{9,8},{10,9},{11,10},{13,12},{... | collective-permute-start | bytes 12296 | tf_op jit(solution)/shard_map/ppermute | solution.py:29
  420.5 15.2 %collective-permute-start.60 = (f32[1,32,32,128]{3,2,1,0:T(8,128)S(1)}, f32[1,32,32,128]{3,2,1,0:T(8,128)S(1)}, u32[]{:S(2)}, u32[]{:S(2)}) collective-permute-start(f32[1,32,32,128]{3,2,1,0:T(8,128)S(1)} %fusion.75), channel_id=1, source_target_pairs={{0,4},{4,8},{8,12},{12,16},{16,20},{20,24},{24,28},{1,5},{5,9},{9,... | collective-permute-start | bytes 1572872 | tf_op jit(solution)/shard_map/ppermute | solution.py:18
  424.5 10.5 %collective-permute-start.62 = (f32[1,32,32,1]{3,2,1,0:T(8,128)S(1)}, f32[1,32,32,1]{3,2,1,0:T(8,128)S(1)}, u32[]{:S(2)}, u32[]{:S(2)}) collective-permute-start(f32[1,32,32,1]{3,2,1,0:T(8,128)S(1)} %get-tuple-element.37), channel_id=1, source_target_pairs={{1,0},{2,1},{3,2},{5,4},{6,5},{7,6},{9,8},{10,9},{11,10},{13,12},{... | collective-permute-start | bytes 12296 | tf_op jit(solution)/shard_map/ppermute | solution.py:29
  438.0 18.5 %collective-permute-start.63 = (f32[1,32,32,128]{3,2,1,0:T(8,128)}, f32[1,32,32,128]{3,2,1,0:T(8,128)}, u32[]{:S(2)}, u32[]{:S(2)}) collective-permute-start(f32[1,32,32,128]{3,2,1,0:T(8,128)} %get-tuple-element.21), channel_id=1, source_target_pairs={{0,4},{4,8},{8,12},{12,16},{16,20},{20,24},{24,28},{1,5},{5,9},{9,... | collective-permute-start | bytes 1572872 | tf_op jit(solution)/shard_map/ppermute | solution.py:18
  461.1 17.0 %collective-permute-start.66 = (f32[1,32,32,128]{3,2,1,0:T(8,128)}, f32[1,32,32,128]{3,2,1,0:T(8,128)}, u32[]{:S(2)}, u32[]{:S(2)}) collective-permute-start(f32[1,32,32,128]{3,2,1,0:T(8,128)} %get-tuple-element.17), channel_id=1, source_target_pairs={{0,4},{4,8},{8,12},{12,16},{16,20},{20,24},{24,28},{1,5},{5,9},{9,... | collective-permute-start | bytes 1572872 | tf_op jit(solution)/shard_map/ppermute | solution.py:18
  483.5 19.6 %collective-permute-start.69 = (f32[1,32,32,128]{3,2,1,0:T(8,128)}, f32[1,32,32,128]{3,2,1,0:T(8,128)}, u32[]{:S(2)}, u32[]{:S(2)}) collective-permute-start(f32[1,32,32,128]{3,2,1,0:T(8,128)} %get-tuple-element.13), channel_id=1, source_target_pairs={{0,4},{4,8},{8,12},{12,16},{16,20},{20,24},{24,28},{1,5},{5,9},{9,... | collective-permute-start | bytes 1572872 | tf_op jit(solution)/shard_map/ppermute | solution.py:18
  (50 other events, 316.4 us)
where the time goes:
time: 518 us; the launch traced here: 508 us
  starting transfers between devices  233 us (45%)
  waiting for transfers between devices  155 us (30%)
  other arithmetic  68.7 us (13%)
  local copies, waits for them, and re-layouts  48.5 us (9%)
    ppermute x25, starting transfers between devices, passed_along(): return lax.ppermute(block, axis, route)  111 us
    ppermute x22, waiting for transfers between devices, padded_2(): lax.ppermute(lax.slice_in_dim(block, 0, width, axis=dim), axis, backward)  67.6 us
    ppermute x22, starting transfers between devices, padded_2(): lax.ppermute(lax.slice_in_dim(block, 0, width, axis=dim), axis, backward)  63.9 us
    ppermute x22, starting transfers between devices, padded_2(): lax.ppermute(lax.slice_in_dim(block, block.shape[dim] - width, None, axis...  58 us
    ppermute x22, waiting for transfers between devices, padded_2(): lax.ppermute(lax.slice_in_dim(block, block.shape[dim] - width, None, axis...  42.9 us
    concatenate x22, other arithmetic, padded_2(): block = jnp.concatenate([low, block, high], axis=dim)  27.7 us
    ppermute x3, waiting for transfers between devices, partner(): return lax.ppermute(block, axis, route)  24.7 us
    add x13, other arithmetic, smooth_single(): values + scaled * (target - operate(values, diffusivity, time_coef, stride))  24.2 us
  transfers between devices with their start and end apart: 72, of which 38 were waited for; matrix products, arithmetic and copies ran while one was open for 15% of the time, Pallas kernels for 0%

commit v1 on v0

v1 whole, which is shorter than its diff:
```python
import jax
import jax.numpy as jnp
from jax import lax
from jax.experimental import pallas as pl
from jax.experimental.pallas import tpu as pltpu
from jax.sharding import PartitionSpec as P

LEVELS = 5
damping = 0.8
base_coef = 8.0
F32 = jnp.float32
MESH = pl.DeviceIdType.MESH
PAD = 8


def make(mesh, nt, nx, ny, nz):
    ntm, ngz = mesh.shape["tm"], mesh.shape["gz"]
    group = 2 ** (LEVELS - 1) // nt
    groups = ntm // group
    half = group // 2
    xb = nx // group
    yp = ny + 2 * PAD
    hi0 = nz // 2
    times = [0] + [group // 2**l for l in range(LEVELS - 1)]
    versions = [0] + [4] * (LEVELS - 2) + [3]
    n_coarse = sum(versions)

    def kernel(src, guess, dif_hbm, sol, res, *scr):
        scr = list(scr)
        V = [scr.pop(0) for _ in range(6)]
        PV = [scr.pop(0) for _ in range(6)]
        f, dif, S0, rb, g1, es, rout = [scr.pop(0) for _ in range(7)]
        A = [None] + [[scr.pop(0) for _ in range(versions[l])] for l in range(1, LEVELS)]
        G = [None] + [scr.pop(0) for _ in range(1, LEVELS)]
        E = [None] + [scr.pop(0) for _ in range(1, LEVELS)]
        S = [S0] + [scr.pop(0) for _ in range(1, LEVELS)]
        ZS, ZL, ZR = [scr.pop(0) for _ in range(3)]
        (load_sem, out_sem, zsend, zlr, zrr, xsend, xlr, xrr, usend, urecv,
         asend, arecv, esend, erecv, psend, precv, tsend, trecv) = scr

        tm, gz = lax.axis_index("tm"), lax.axis_index("gz")
        grp, i = lax.div(tm, group), lax.rem(tm, group)

        def pos_of(k):
            return jnp.where(lax.rem(k, 2) == 0, lax.div(k, 2), group - 1 - lax.div(k, 2))

        def index_of(p):
            return jnp.where(p < half, 2 * p, 2 * (group - 1 - p) + 1)

        p = pos_of(i)
        center = pl.ds(PAD, ny)

        loads = [
            pltpu.make_async_copy(guess, V[0].at[:, pl.ds(1, nx), center, :], load_sem.at[0]),
            pltpu.make_async_copy(src, f, load_sem.at[1]),
            pltpu.make_async_copy(dif_hbm, dif, load_sem.at[2]),
        ]
        for c in loads:
            c.start()

        zpad = jnp.zeros((PAD, nz), F32)
        zrow = jnp.zeros((ny, nz), F32)

        for t in range(nt):
            def clear0(x, _, t=t):
                for v in V:
                    v[t, x, pl.ds(0, PAD), :] = zpad
                    v[t, x, pl.ds(PAD + ny, PAD), :] = zpad
                return 0
            lax.fori_loop(0, nx + 2, clear0, 0)
            for v in V:
                v[t, 0, center, :] = zrow
                v[t, nx + 1, center, :] = zrow
        for l in range(1, LEVELS):
            def clear1(t, _, l=l):
                for a in A[l]:
                    for x in range(xb + 2):
                        a[t, x] = jnp.zeros((yp, nz), F32)
                return 0
            lax.fori_loop(0, times[l] + 1, clear1, 0)

        @pl.when(tm == 0)
        def _():
            def clear2(x, _):
                for v in PV:
                    v[x] = zrow
                return 0
            lax.fori_loop(0, nx, clear2, 0)

        def clear3(n, _):
            ZL[n] = zrow
            ZR[n] = zrow
            return 0
        lax.fori_loop(0, 12 + n_coarse, clear3, 0)

        bar = pltpu.get_barrier_semaphore()

        def greet(where):
            pl.semaphore_signal(bar, inc=1, device_id=where, device_id_type=MESH)

        for j in range(1, group):
            greet({"tm": grp * group + lax.rem(i + j, group)})
        met = group - 1
        for d in (-1, 1):
            there = (gz + d >= 0) & (gz + d < ngz)
            met = met + jnp.where(there, 1, 0)

            @pl.when(there)
            def _(d=d):
                greet({"gz": gz + d})
        if groups > 1:
            for d in (-1, 1):
                there = (grp + d >= 0) & (grp + d < groups)
                met = met + jnp.where(there, group, 0)

                @pl.when(there)
                def _(d=d):
                    for j in range(group):
                        greet({"tm": (grp + d) * group + j})
        pl.semaphore_wait(bar, met)

        def remote(s, d, ss, rs, where):
            return pltpu.make_async_remote_copy(
                src_ref=s, dst_ref=d, send_sem=ss, recv_sem=rs, device_id=where, device_id_type=MESH)

        def step_copy(n, source):
            return remote(source, PV[n], usend.at[n], urecv.at[n], {"tm": tm + 1})

        def step_send(n, source):
            @pl.when(tm < ntm - 1)
            def _():
                step_copy(n, source).start()

        def step_recv(n, source):
            @pl.when(tm > 0)
            def _():
                step_copy(n, source).wait_recv()

        def step_sent(n, source):
            @pl.when(tm < ntm - 1)
            def _():
                step_copy(n, source).wait_send()

        def z_copies(n):
            par = n % 2
            return (remote(ZS.at[n], ZR.at[n], zsend.at[0, par], zrr.at[n], {"gz": gz - 1}),
                    remote(ZS.at[n], ZL.at[n], zsend.at[1, par], zlr.at[n], {"gz": gz + 1}))

        def z_send(n):
            lo, hi = z_copies(n)

            @pl.when(gz > 0)
            def _():
                lo.start()

            @pl.when(gz < ngz - 1)
            def _():
                hi.start()

        def z_wait(n):
            lo, hi = z_copies(n)

            @pl.when(gz > 0)
            def _():
                lo.wait_send()
                hi.wait_recv()

            @pl.when(gz < ngz - 1)
            def _():
                hi.wait_send()
                lo.wait_recv()

        lane = lax.broadcasted_iota(jnp.int32, (ny, nz), 1)

        def pack(acc, val, k):
            acc = jnp.where(lane == k, pltpu.roll(val, k, 1), acc)
            return jnp.where(lane == hi0 + k, pltpu.roll(val, lax.rem(k + hi0 + 1, nz), 1), acc)

        def flux(v, t, x, n, k):
            c = v[t, x, center, :]
            nb = v[t, x + 1, center, :] + v[t, x - 1, center, :]
            nb = nb + v[t, x, pl.ds(PAD + 1, ny), :] + v[t, x, pl.ds(PAD - 1, ny), :]
            left = jnp.where(lane == 0, pltpu.roll(ZL[n], hi0 - k, 1), pltpu.roll(c, 1, 1))
            right = jnp.where(lane == nz - 1, pltpu.roll(ZR[n], nz - 1 - k, 1), pltpu.roll(c, nz - 1, 1))
            return c, 6.0 * c - (nb + right + left)

        def defect(v, t, x, n, k, before, target, d, coef):
            c, lap = flux(v, t, x, n, k)
            return c, target - (coef * (c - before) + d * lap)

        def run(count, fn, n):
            def step(k, acc):
                return pack(acc, fn(k), k)
            ZS[n] = lax.fori_loop(0, count, step, zrow, unroll=2)
            z_send(n)

        def each(count, fn):
            def step(k, _):
                fn(k)
                return 0
            lax.fori_loop(0, count, step, 0, unroll=2)

        def before0(m, pn, t, x):
            return PV[pn][x] if t == 0 else V[m][t - 1, x + 1, center, :]

        def sweep0(m, t):
            n = 2 * m + t

            def fn(x):
                c, r = defect(V[m], t, x + 1, n, x, before0(m, m, t, x), f[t, x], dif[x], base_coef)
                new = c + S0[x] * r
                V[m + 1][t, x + 1, center, :] = new
                return new
            run(nx, fn, n + 2)

        def resid0(m, t, put):
            n = 2 * m + t

            def fn(x):
                _, r = defect(V[m], t, x + 1, n, x, before0(m, m, t, x), f[t, x], dif[x], base_coef)
                put(x, r)
            each(nx, fn)

        last = nt - 1

        def block(m):
            return V[m].at[last, pl.ds(1, nx), center, :]

        step_send(0, guess.at[last])
        for c in loads:
            c.wait()

        for t in (1, 0):
            def first(x, t=t):
                return V[0][t, x + 1, center, :]
            run(nx, first, t)

        def scales(x):
            S0[x] = damping / (base_coef + 6.0 * dif[x])
        each(nx, scales)
        for l in range(1, LEVELS):
            for x in range(xb):
                S[l][x] = damping / (base_coef / 2.0**l + 6.0 * dif[p * xb + x])

        z_wait(1)
        sweep0(0, 1)
        step_send(1, block(1))
        step_recv(0, guess.at[last])
        z_wait(0)
        sweep0(0, 0)
        z_wait(3)
        sweep0(1, 1)
        step_send(2, block(2))
        step_recv(1, block(1))
        z_wait(2)
        sweep0(1, 0)

        def put_rb(x, r):
            rb[x] = r
        z_wait(5)
        resid0(2, 1, put_rb)
        z_wait(4)
        step_recv(2, block(2))

        def put_g(x, r):
            g1[x] = (r + rb[x]) * 0.5
        resid0(2, 0, put_g)
        step_sent(0, guess.at[last])
        step_sent(1, block(1))
        step_sent(2, block(2))

        def a2a(j, to):
            other = lax.rem(i + j, group)
            return remote(g1.at[pl.ds(pos_of(other) * xb, xb)], G[1].at[to], asend.at[j], arecv.at[j],
                          {"tm": grp * group + other})

        for j in range(1, group):
            a2a(j, i).start()
        for x in range(xb):
            G[1][i, x] = g1[p * xb + x]
        for j in range(1, group):
            c = a2a(j, lax.rem(i + group - j, group))
            c.wait_recv()
            c.wait_send()

        slot = [0]

        def halo_copies(l, ver, n):
            a, T = A[l][ver], times[l]
            steps = pl.ds(1, T)
            lo = remote(a.at[steps, 1, center, :], a.at[steps, xb + 1, center, :],
                        xsend.at[0], xrr.at[n], {"tm": grp * group + index_of(lax.max(p - 1, 0))})
            hi = remote(a.at[steps, xb, center, :], a.at[steps, 0, center, :],
                        xsend.at[1], xlr.at[n], {"tm": grp * group + index_of(lax.min(p + 1, group - 1))})
            nxt = None
            if groups > 1:
                nxt = remote(a.at[T, pl.ds(1, xb), center, :], a.at[0, pl.ds(1, xb), center, :],
                             tsend.at[0], trecv.at[n], {"tm": tm + group})
            return lo, hi, nxt

        def fill(l, ver, fn):
            n = slot[0]
            slot[0] += 1
            T = times[l]
            a = A[l][ver]

            def put(k):
                t, x = lax.div(k, xb), lax.rem(k, xb)
                val = fn(t, x, k)
                a[t + 1, x + 1, center, :] = val
                return val
            run(T * xb, put, 12 + n)
            lo, hi, nxt = halo_copies(l, ver, n)

            @pl.when(p > 0)
            def _():
                lo.start()

            @pl.when(p < group - 1)
            def _():
                hi.start()
            if nxt is not None:
                @pl.when(grp < groups - 1)
                def _():
                    nxt.start()
            z_wait(12 + n)

            @pl.when(p > 0)
            def _():
                lo.wait_send()
                hi.wait_recv()

            @pl.when(p < group - 1)
            def _():
                hi.wait_send()
                lo.wait_recv()
            if nxt is not None:
                @pl.when(grp < groups - 1)
                def _():
                    nxt.wait_send()

                @pl.when(grp > 0)
                def _():
                    nxt.wait_recv()
            return 12 + n

        def defect_at(l, ver, n, t, x, k):
            a = A[l][ver]
            return defect(a, t + 1, x + 1, n, k, a[t, x + 1, center, :], G[l][t, x], dif[p * xb + x],
                          base_coef / 2.0**l)

        def relaxed(l, ver, n):
            def fn(t, x, k):
                c, r = defect_at(l, ver, n, t, x, k)
                return c + S[l][x] * r
            return fn

        def finish(l, ver, n):
            fn = relaxed(l, ver, n)

            def put(k):
                t, x = lax.div(k, xb), lax.rem(k, xb)
                E[l][t, x] = fn(t, x, k)
            each(times[l] * xb, put)

        def coarse(l):
            n = fill(l, 0, lambda t, x, k: S[l][x] * G[l][t, x])
            n = fill(l, 1, relaxed(l, 0, n))
            if l == LEVELS - 1:
                n = fill(l, 2, relaxed(l, 1, n))
                finish(l, 2, n)
                return

            def down(k):
                t, x = lax.div(k, xb), lax.rem(k, xb)
                _, ra = defect_at(l, 1, n, 2 * t, x, 2 * t * xb + x)
                _, rc = defect_at(l, 1, n, 2 * t + 1, x, (2 * t + 1) * xb + x)
                G[l + 1][t, x] = (ra + rc) * 0.5
            each(times[l + 1] * xb, down)
            coarse(l + 1)
            n = fill(l, 2, lambda t, x, k: A[l][1][t + 1, x + 1, center, :] + E[l + 1][lax.div(t, 2), x])
            n = fill(l, 3, relaxed(l, 2, n))
            finish(l, 3, n)

        coarse(1)

        ep = PV[5]

        def back(j, at):
            other = lax.rem(i + j, group)
            return remote(E[1].at[other], es.at[pl.ds(at * xb, xb)], esend.at[j], erecv.at[j],
                          {"tm": grp * group + other})

        def ahead(j, at):
            other = lax.rem(i + j, group)
            return other, remote(E[1].at[lax.rem(other + group - 1, group)], ep.at[pl.ds(at * xb, xb)],
                                 psend.at[j], precv.at[j],
                                 {"tm": jnp.where(other == 0, grp + 1, grp) * group + other})

        for j in range(1, group):
            back(j, p).start()
        for j in range(group):
            other, c = ahead(j, p)
            if j > 0:
                @pl.when(other > 0)
                def _(c=c):
                    c.start()
            if groups > 1:
                @pl.when((other == 0) & (grp < groups - 1))
                def _(c=c):
                    c.start()
        for x in range(xb):
            es[p * xb + x] = E[1][i, x]

        @pl.when(i > 0)
        def _():
            for x in range(xb):
                ep[p * xb + x] = E[1][lax.max(i - 1, 0), x]
        for j in range(1, group):
            back(j, pos_of(lax.rem(i + group - j, group))).wait_recv()

        for t in (1, 0):
            def lift(x, t=t):
                val = V[2][t, x + 1, center, :] + es[x]
                V[3][t, x + 1, center, :] = val
                return val
            run(nx, lift, 6 + t)
        z_wait(7)
        sweep0(3, 1)
        step_send(3, block(4))
        for j in range(group):
            _, c = ahead(j, pos_of(lax.rem(i + group - j, group)))
            if j > 0:
                @pl.when(i > 0)
                def _(c=c):
                    c.wait_recv()
            if groups > 1:
                @pl.when((i == 0) & (grp > 0))
                def _(c=c):
                    c.wait_recv()

        def lift_prev(x):
            rb[x] = PV[2][x] + ep[x]
        each(nx, lift_prev)
        z_wait(6)

        def sweep_a(m, prev):
            n = 2 * m

            def fn(x):
                c, r = defect(V[m], 0, x + 1, n, x, prev[x], f[0, x], dif[x], base_coef)
                new = c + S0[x] * r
                V[m + 1][0, x + 1, center, :] = new
                return new
            run(nx, fn, n + 2)

        sweep_a(3, rb)
        z_wait(9)
        sweep0(4, 1)
        step_send(4, block(5))
        outs = [pltpu.make_async_copy(V[5].at[t, pl.ds(1, nx), center, :], sol.at[t], out_sem.at[t])
                for t in range(nt)]
        outs[1].start()
        step_recv(3, block(4))
        z_wait(8)
        sweep_a(4, PV[3])
        outs[0].start()
        z_wait(11)

        def put_r(t):
            def put(x, r):
                rout[t, x] = r
            return put
        resid0(5, 1, put_r(1))
        rcopy = [pltpu.make_async_copy(rout.at[t], res.at[t], out_sem.at[nt + t]) for t in range(nt)]
        rcopy[1].start()
        z_wait(10)
        step_recv(4, block(5))

        def last_res(x):
            _, r = defect(V[5], 0, x + 1, 10, x, PV[4][x], f[0, x], dif[x], base_coef)
            rout[0, x] = r
        each(nx, last_res)
        rcopy[0].start()
        step_sent(3, block(4))
        step_sent(4, block(5))
        for j in range(1, group):
            back(j, p).wait_send()
        for j in range(group):
            other, c = ahead(j, p)
            if j > 0:
                @pl.when(other > 0)
                def _(c=c):
                    c.wait_send()
            if groups > 1:
                @pl.when((other == 0) & (grp < groups - 1))
                def _(c=c):
                    c.wait_send()
        for c in outs + rcopy:
            c.wait()

    full = pltpu.VMEM((nx, ny, nz), F32)
    dma = pltpu.SemaphoreType.DMA
    nzs = 12 + n_coarse
    scratch = [pltpu.VMEM((nt, nx + 2, yp, nz), F32)] * 6 + [full] * 6
    scratch += [pltpu.VMEM((nt, nx, ny, nz), F32), full, full, full, full, full, pltpu.VMEM((nt, nx, ny, nz), F32)]
    for l in range(1, LEVELS):
        scratch += [pltpu.VMEM((times[l] + 1, xb + 2, yp, nz), F32)] * versions[l]
    scratch += [pltpu.VMEM((times[l], xb, ny, nz), F32) for l in range(1, LEVELS)] * 2
    scratch += [pltpu.VMEM((xb, ny, nz), F32)] * (LEVELS - 1)
    scratch += [pltpu.VMEM((nzs, ny, nz), F32)] * 3
    scratch += [dma((3,)), dma((2 * nt,)), dma((2, 2)), dma((nzs,)), dma((nzs,)), dma((2,)), dma((n_coarse,)),
                dma((n_coarse,)), dma((5,)), dma((5,))] + [dma((group,))] * 6 + [dma((1,)), dma((n_coarse,))]
    shape = jax.ShapeDtypeStruct((nt, nx, ny, nz), F32)
    anyspec = pl.BlockSpec(memory_space=pl.ANY)
    return pl.pallas_call(
        kernel,
        out_shape=(shape, shape),
        in_specs=[anyspec] * 3,
        out_specs=(anyspec, anyspec),
        scratch_shapes=scratch,
        compiler_params=pltpu.CompilerParams(collective_id=0, has_side_effects=True, vmem_limit_bytes=56 << 20),
    )


def solution(mesh):
    def body(source, initial_guess, diffusivity):
        return make(mesh, *source.shape)(source, initial_guess, diffusivity)

    placed = (P("tm", None, None, "gz"), P("tm", None, None, "gz"), P(None, None, "gz"))
    return jax.shard_map(
        body,
        mesh=mesh,
        in_specs=placed,
        out_specs=(P("tm", None, None, "gz"), P("tm", None, None, "gz")),
        check_vma=False,
    )
```

time: 518 us -> 181 us (0.35)
  the two profiles are of different devices: /device:TPU:1 before, /device:TPU:27 now
where the time goes in v1:
time: 181 us
  Pallas kernels  177 us (98%)
  local copies, waits for them, and re-layouts  3.32 us (2%)
    pallas_call x1, Pallas kernels, body(): return make(mesh, *source.shape)(source, initial_guess, diffusivity)  177 us

profile of v1, /device:TPU:27, one launch (start us, length us, event | category | flops | bytes accessed | tf_op | source)
XLA Modules:
  0.0 181.0 jit_solution(13508870728868036581)
XLA Ops:
  0.6 177.0 %shard_map.50 = (f32[2,32,32,128]{3,2,1,0:T(8,128)}, f32[2,32,32,128]{3,2,1,0:T(8,128)}) custom-call(f32[2,32,32,128]{3,2,1,0:T(8,128)} %src.1, f32[2,32,32,128]{3,2,1,0:T(8,128)} %guess.1, f32[32,32,128]{2,1,0:T(8,128)} %dif_hbm.1), custom_call_target="tpu_custom_call" | custom-call | tf_op jit(solution)/shard_map/pallas_call | solution.py:528
  177.7 0.0 copy-start
  177.7 2.4 %copy.7 = f32[2,32,32,128]{3,2,1,0:T(8,128)} copy(f32[2,32,32,128]{3,2,1,0:T(8,128)} %get-tuple-element.4) | data formatting | bytes 2097152
  180.0 0.0 copy-done
  180.0 1.0 copy.8
Async XLA Ops:
  177.7 2.4 %copy-start = (f32[2,32,32,128]{3,2,1,0:T(8,128)S(1)}, f32[2,32,32,128]{3,2,1,0:T(8,128)}, u32[]{:S(2)}) copy-start(f32[2,32,32,128]{3,2,1,0:T(8,128)} %get-tuple-element.5) | copy-start | bytes 3145732
